TPU v7x, 768 devices: a whole 4x8x12 slice. The times are simulated.
768 devices in a mesh: dp: 24 (over z, core), section: 4 (over x), head: 8 (over y).
Axes of the slice: x: 4, y: 8, z: 12, core: 2. Of those that a mesh axis runs over, the one named last changes fastest.
Arguments:
- q_latent: bfloat16 [4, 12288, 1536], P('section', 'dp'), may hold values from -6 to 6
- kv_latent: bfloat16 [4, 12288, 576], P('section', 'dp'), may hold values from -6 to 6
- segment_ids: int32 [12288], P('dp'), may hold values from 0 to 191, never falling along the last dimension, each value on 1 to 512 neighbouring positions
- q_weight: bfloat16 [4, 1536, 12288], P('section', 'dp', 'head'), may hold values from -100 to 100
- k_weight: bfloat16 [4, 512, 8192], P('section', None, 'head'), may hold values from -0.25 to 0.25
Outputs:
- logit_ratio: float32 [4, 64], P(None, 'head')
- scaled_q: bfloat16 [4, 1536, 12288], P('section', 'dp', 'head')
- scaled_k: bfloat16 [4, 512, 8192], P('section', None, 'head')
All inputs are finite; a program needn't handle non-finite values.
Results may differ from a plain program's by a relative error of at most 0.0034.
Values may be sent and summed in bfloat16 or wider, within the bound.
No kernel may reach another device: no remote copies, remote signals or barrier semaphores. Data moves between devices by JAX's collectives and lax.ppermute only.
A program may use at most 32 MiB of HBM per device.

v0:
```python
import jax
import jax.numpy as jnp
from jax import lax
from jax.sharding import PartitionSpec as P

D_KV = 512
NOPE = 128
ROPE = 64


clip_threshold = 100.0
rope_base = 50000.0


def copy_for_each(value, axis):
    count = lax.axis_size(axis)
    return lax.all_to_all(
        jnp.broadcast_to(value[None], (count, *value.shape)), axis, 0, 0, tiled=True
    )


def over_copies(value, axis):
    everything = copy_for_each(value, axis)
    return jnp.max(everything, axis=0)


def joined_along(parts, dim):
    parts = jnp.moveaxis(parts, 0, dim)
    dims = parts.shape
    return parts.reshape(*dims[:dim], dims[dim] * dims[dim + 1], *dims[dim + 2 :])


def gather_directly(value, axis, dim):
    parts = copy_for_each(value, axis)
    return joined_along(parts, dim)


def rotate(values, positions):
    half_width = values.shape[-1] // 2
    frequency = rope_base ** (-jnp.arange(half_width, dtype=jnp.float32) / half_width)
    angles = positions[:, None].astype(jnp.float32) * frequency[None, :]
    cosine = jnp.cos(angles)[:, None, :]
    sine_part = jnp.sin(angles)[:, None, :]
    lower_half = values[..., :half_width]
    upper_half = values[..., half_width:]
    return jnp.concatenate(
        [
            lower_half * cosine - upper_half * sine_part,
            upper_half * cosine + lower_half * sine_part,
        ],
        -1,
    )


def sequence_maxima(q_full, kv_rows, segments, w_key):
    length = kv_rows.shape[0]
    heads_here = w_key.shape[1] // NOPE
    q_full = q_full.reshape(length, heads_here, NOPE + ROPE)
    positions = jnp.arange(length, dtype=jnp.int32)
    queries = jnp.concatenate(
        [q_full[..., :NOPE], rotate(q_full[..., NOPE:], positions)], -1
    ).astype(jnp.bfloat16)
    key_nope = jnp.dot(kv_rows[:, :D_KV], w_key, preferred_element_type=jnp.float32).astype(
        jnp.bfloat16
    )
    key_nope = key_nope.reshape(length, heads_here, NOPE)
    key_rope = jnp.broadcast_to(kv_rows[:, None, D_KV:], (length, heads_here, ROPE))
    keys_all = jnp.concatenate([key_nope, key_rope], -1)
    logits = jnp.einsum("shd,thd->hst", queries, keys_all, preferred_element_type=jnp.float32)
    logits = logits * (NOPE + ROPE) ** (-0.5)
    allowed = (segments[:, None] == segments[None, :]) & (positions[None, :] <= positions[:, None])
    return jnp.max(jnp.where(allowed[None], logits, -1e30), axis=(1, 2))


def scale_weights(own_max, q_weight, k_weight):
    factor = clip_threshold / jnp.maximum(own_max, clip_threshold)
    square_root = jnp.sqrt(factor)
    layers_here, heads_here = own_max.shape
    column_scale = jnp.concatenate(
        [
            jnp.broadcast_to(square_root[..., None], (layers_here, heads_here, NOPE)),
            jnp.broadcast_to(factor[..., None], (layers_here, heads_here, ROPE)),
        ],
        -1,
    )
    rows_q = q_weight.shape[1]
    scaled_q = (
        (
            q_weight.astype(jnp.float32).reshape(layers_here, rows_q, heads_here, NOPE + ROPE)
            * column_scale[:, None]
        )
        .reshape(q_weight.shape)
        .astype(jnp.bfloat16)
    )
    scaled_k = (
        (
            k_weight.astype(jnp.float32).reshape(layers_here, D_KV, heads_here, NOPE)
            * square_root[:, None, :, None]
        )
        .reshape(k_weight.shape)
        .astype(jnp.bfloat16)
    )
    return (scaled_q, scaled_k)


def per_device(q_latent, kv_latent, segment_ids, q_weight, k_weight):
    latent_q = q_latent[0]
    q_full = jnp.dot(
        latent_q,
        lax.all_gather(q_weight[0], "dp", axis=0, tiled=True),
        preferred_element_type=jnp.float32,
    )
    own_rows = [sequence_maxima(q_full, kv_latent[0], segment_ids, k_weight[0])]
    own_max = jnp.stack(own_rows)
    layer_max = over_copies(own_max, "dp")
    max_table = gather_directly(layer_max, "section", 0)
    scaled_q, scaled_k = scale_weights(layer_max, q_weight, k_weight)
    return (max_table / clip_threshold, scaled_q, scaled_k)


def solution(mesh):
    return jax.shard_map(
        per_device,
        mesh=mesh,
        in_specs=(
            P("section", "dp", None),
            P("section", "dp", None),
            P("dp"),
            P("section", "dp", "head"),
            P("section", None, "head"),
        ),
        out_specs=(P(None, "head"), P("section", "dp", "head"), P("section", None, "head")),
        check_vma=False,
    )
```

profile of v0, /device:TPU:1, one launch (start us, length us, event | category | flops | bytes accessed | tf_op | source)
XLA Modules:
  0.0 127.6 jit_solution(12754551740550627850)
XLA Ops:
  7.2 0.0 copy-start
  7.2 0.0 copy-start.4
  7.2 0.0 all-gather.3.cloned.1.call-start
  7.2 0.7 all-gather.3.cloned.1.call-update
  7.9 0.8 slice.28
  8.8 2.1 %convolution_convert_fusion = bf16[512,1024]{1,0:T(8,128)(2,1)S(1)} fusion(bf16[1,512,1024]{2,1,0:T(8,128)(2,1)} %param.9, bf16[512,576]{0,1:T(8,128)(2,1)} %bitcast.21), kind=kOutput, calls=%fused_computation.13 | convolution fusion | flops 537395200 | bytes 2621440 | tf_op jit(solution)/shard_map/dot_general | solution.py:63
  10.9 1.3 %copy.17 = bf16[512,1024]{0,1:T(8,128)(2,1)} copy(bf16[512,1024]{1,0:T(8,128)(2,1)S(1)} %convolution_convert_fusion) | data formatting | bytes 2097152 | tf_op jit(solution)/shard_map/reshape | solution.py:66
  12.2 0.3 multiply_cosine_fusion
  12.5 0.0 copy-done.4
  12.6 0.2 fusion.11
  12.8 68.6 %all-gather.3.cloned.1.call-done = bf16[1,1536,1536]{2,1,0:T(8,128)(2,1)} async-done(((bf16[1,64,1536]{2,1,0:T(8,128)(2,1)}), bf16[1,1536,1536]{2,1,0:T(8,128)(2,1)}) %all-gather.3.cloned.1.call-update) | async-done | bytes 4718608 | tf_op jit(solution)/shard_map/all_gather | solution.py:110
  81.3 6.7 %copy.14 = bf16[1536,1536]{1,0:T(8,128)(2,1)} copy(bf16[1536,1536]{0,1:T(8,128)(2,1)} %bitcast.17) | data formatting | bytes 9437184 | tf_op jit(solution)/shard_map/dot_general | solution.py:108
  88.0 0.0 copy-done
  88.0 4.5 %fusion.8 = f32[512,8,192]{0,2,1:T(8,128)S(1)} fusion(bf16[8,192,1536]{2,1,0:T(8,128)(2,1)} %bitcast.18, bf16[1,512,1536]{2,1,0:T(8,128)(2,1)S(1)} %copy-done), kind=kOutput, calls=%fused_computation.11 | convolution fusion | flops 2415919104 | bytes 9437184 | tf_op jit(solution)/shard_map/dot_general | solution.py:108
  92.6 0.0 copy-start.2
  92.6 0.1 slice.36
  92.7 0.2 subtract_convert_fusion
  93.0 0.9 copy-done.2
  93.8 0.0 copy-start.3
  93.8 0.0 copy-start.1
  93.8 2.1 %select_reduce_fusion = f32[8]{0:T(128)S(1)} fusion(pred[512,512]{1,0:T(8,128)(4,1)S(1)} %fusion.11, bf16[512,8,32]{0,2,1:T(8,128)(2,1)S(1)} %get-tuple-element.6, bf16[512,8,32]{0,2,1:T(8,128)(2,1)S(1)} %get-tuple-element.5, bf16[512,8,128]{0,2,1:T(8,128)(2,1)S(1)} %slice.36, bf16[512,8,64]{0,2,1:T(8,128)(2,1)S(1)} %broadcast_in_dim.23, ...), kind=kOutput, calls=%fused_computation | convolution fusion | flops 819462144 | bytes 3407904 | tf_op jit(solution)/shard_map/shd,thd->hst/dot_general | solution.py:69
  95.9 15.3 %all_to_all.10 = f32[24,1,8]{2,1,0:T(1,128)S(1)} all-to-all(f32[24,1,8]{2,1,0:T(1,128)S(1)} %broadcast_in_dim.25), channel_id=1, replica_groups=mesh['dp'=24,'section'=4,'head'=8] {'dp'}, dimensions={0} | all-to-all | bytes 1536 | tf_op jit(solution)/shard_map/all_to_all | solution.py:17
  111.3 0.1 broadcast_bitcast_fusion
  111.4 0.1 broadcast_in_dim.28
  111.4 0.1 broadcast_in_dim.27
  111.5 0.1 mul.117
  111.6 0.6 broadcast_in_dim.26
  112.2 4.0 %all-to-all-start.1 = ((f32[4,1,8]{2,1,0:T(1,128)}), f32[4,1,8]{2,1,0:T(1,128)S(1)}, u32[]{:S(2)}, u32[]{:S(2)}) async-start(f32[4,1,8]{2,1,0:T(1,128)} %broadcast_in_dim.26), calls=%async_computation.1 | async-start | bytes 4096 | tf_op jit(solution)/shard_map/all_to_all | solution.py:17
  116.1 0.0 copy-done.3
  116.1 0.7 multiply_convert_fusion.1
  116.8 0.0 copy-done.1
  116.8 1.2 multiply_convert_fusion
  118.1 2.1 %all-to-all-done.1 = f32[4,1,8]{2,1,0:T(1,128)S(1)} async-done(((f32[4,1,8]{2,1,0:T(1,128)}), f32[4,1,8]{2,1,0:T(1,128)S(1)}, u32[]{:S(2)}, u32[]{:S(2)}) %all-to-all-start.1) | async-done | bytes 160 | tf_op jit(solution)/shard_map/all_to_all | solution.py:17
  120.2 0.6 broadcast_multiply_fusion
  (7 shorter events, 0.1 us)
Async XLA Ops:
  7.2 80.9 %copy-start = (bf16[1,512,1536]{2,1,0:T(8,128)(2,1)S(1)}, bf16[1,512,1536]{2,1,0:T(8,128)(2,1)}, u32[]{:S(2)}) copy-start(bf16[1,512,1536]{2,1,0:T(8,128)(2,1)} %param.5) | copy-start | bytes 4718596
  7.2 5.4 %copy-start.4 = (s32[512]{0:T(512)S(1)}, s32[512]{0:T(512)}, u32[]{:S(2)}) copy-start(s32[512]{0:T(512)} %param.7) | copy-start | bytes 6148
  7.2 74.2 %all-gather.3.cloned.1.call-start = ((), (), s32[]{:S(2)}) async-start(), calls=%async_computation.2 | async-start | bytes 4915200 | tf_op jit(solution)/shard_map/all_gather | solution.py:110
  92.6 1.2 copy-start.2
  93.8 22.3 %copy-start.3 = (bf16[1,64,1536]{2,1,0:T(8,128)(2,1)S(1)}, bf16[1,64,1536]{2,1,0:T(8,128)(2,1)}, u32[]{:S(2)}) copy-start(bf16[1,64,1536]{2,1,0:T(8,128)(2,1)} %param.8) | copy-start | bytes 589828
  93.8 23.0 %copy-start.1 = (bf16[1,512,1024]{2,1,0:T(8,128)(2,1)S(1)}, bf16[1,512,1024]{2,1,0:T(8,128)(2,1)}, u32[]{:S(2)}) copy-start(bf16[1,512,1024]{2,1,0:T(8,128)(2,1)} %param.9) | copy-start | bytes 3145732
  112.2 8.0 %all-to-all-start.1 = ((f32[4,1,8]{2,1,0:T(1,128)}), f32[4,1,8]{2,1,0:T(1,128)S(1)}, u32[]{:S(2)}, u32[]{:S(2)}) async-start(f32[4,1,8]{2,1,0:T(1,128)} %broadcast_in_dim.26), calls=%async_computation.1 | async-start | bytes 4096 | tf_op jit(solution)/shard_map/all_to_all | solution.py:17
Sparse Core Ops, SparseCore 0:
  10.4 70.8 all-gather.2
where the time goes:
time: 129 us; the launch traced here: 128 us
  waiting for transfers between devices  71.4 us (55%)
  blocking collectives  15.3 us (12%)
  between operations  14.1 us (11%)
  local copies, waits for them, and re-layouts  10.8 us (8%)
  matrix products  8.69 us (7%)
  starting transfers between devices  4 us (3%)
  other arithmetic  3.26 us (3%)
    all_gather x1, waiting for transfers between devices, per_device(): lax.all_gather(q_weight[0], 'dp', axis=0, tiled=True)  68.6 us
    all_to_all x1, blocking collectives, copy_for_each(): lax.all_to_all(jnp.broadcast_to(value[None], (count, *value.shape)), axis...  15.3 us
    dot_general x1, local copies, waits for them, and re-layouts, per_device(): jnp.dot(latent_q, lax.all_gather(q_weight[0], 'dp', axis=0, tiled=True),...  6.7 us
    dot_general x1, matrix products, per_device(): jnp.dot(latent_q, lax.all_gather(q_weight[0], 'dp', axis=0, tiled=True),...  4.52 us
    all_to_all x1, starting transfers between devices, copy_for_each(): lax.all_to_all(jnp.broadcast_to(value[None], (count, *value.shape)), axis...  3.97 us
  transfers between devices with their start and end apart: 2, of which 2 were waited for; matrix products, arithmetic and copies ran while one was open for 5% of the time, Pallas kernels for 0%

commit v1 on v0

v1 whole, which is shorter than its diff:
```python
import jax
import jax.numpy as jnp
import numpy as np
from jax import lax
from jax.experimental import pallas as pl
from jax.experimental.pallas import tpu as pltpu
from jax.sharding import PartitionSpec as P

D_Q = 1536
D_KV = 512
NOPE = 128
ROPE = 64
HEAD = NOPE + ROPE
SEQ = 512

clip_threshold = 100.0
rope_base = 50000.0
wire_scale = 512.0
masked = -1e30


def rope_tables():
    half = ROPE // 2
    frequency = np.float32(rope_base) ** (-np.arange(half, dtype=np.float32) / np.float32(half))
    angles = np.arange(SEQ, dtype=np.float32)[:, None] * frequency[None, :].astype(np.float32)
    cosine = np.cos(angles.astype(np.float64)).astype(np.float32)
    sine = np.sin(angles.astype(np.float64)).astype(np.float32)
    return np.tile(cosine, (1, 4)), np.concatenate([-sine, sine, -sine, sine], 1)


def maxima_kernel(a_ref, w_ref, kv_ref, kw_ref, seg_ref, cos_ref, sin_ref, o_ref, q_ref, kc_ref, bias_ref, top_ref):
    heads = kw_ref.shape[1] // NOPE
    lane = lax.broadcasted_iota(jnp.int32, (SEQ, 128), 1)
    low = lane < 64
    keys = lax.dot_general(
        kw_ref[...], kv_ref[0:D_KV, :], (((0,), (0,)), ((), ())), preferred_element_type=jnp.float32
    ).astype(jnp.bfloat16)
    shared = kv_ref[D_KV : D_KV + ROPE, :]
    nothing = jnp.zeros_like(shared)
    for h in range(heads):
        upper = keys[h * NOPE : h * NOPE + 64]
        lower = keys[h * NOPE + 64 : (h + 1) * NOPE]
        if h % 2 == 0:
            kc_ref[h] = jnp.concatenate([upper, lower, shared, nothing], 0)
        else:
            kc_ref[h] = jnp.concatenate([lower, upper, nothing, shared], 0)
    row = seg_ref[...].astype(jnp.float32)
    column = jnp.transpose(jnp.broadcast_to(row, (128, SEQ)))
    position = lax.broadcasted_iota(jnp.int32, (SEQ, 128), 0)
    for j in range(SEQ // 128):
        here = slice(j * 128, (j + 1) * 128)
        same = column == jnp.broadcast_to(row[:, here], (SEQ, 128))
        bias_ref[:, here] = jnp.where(same & (lane + j * 128 <= position), 0.0, masked)
    width = 4 * HEAD
    for g in range(heads // 4):
        q_ref[...] = jnp.dot(a_ref[...], w_ref[:, g * width : (g + 1) * width], preferred_element_type=jnp.float32)
        for p in range(2):
            first = q_ref[:, p * 384 : p * 384 + 128]
            second = q_ref[:, p * 384 + 128 : p * 384 + 256]
            third = q_ref[:, p * 384 + 256 : p * 384 + 384]
            turn = jnp.where(low, second, third)
            partner = jnp.where(lane % 64 < 32, pltpu.roll(turn, 96, 1), pltpu.roll(turn, 32, 1))
            turned = (turn * cos_ref[...] + partner * sin_ref[...]).astype(jnp.bfloat16)
            swapped = jnp.where(low, third, second)
            for i, part in enumerate((first, swapped)):
                h = 4 * g + 2 * p + i
                query = jnp.concatenate([part.astype(jnp.bfloat16), turned], 1)
                top = None
                for s0, s1, t1 in ((0, 256, 256), (256, 512, 512)):
                    x = jnp.dot(query[s0:s1], kc_ref[h, :, 0:t1], preferred_element_type=jnp.float32)
                    x = x + bias_ref[s0:s1, 0:t1]
                    for t in range(0, t1, 128):
                        y = jnp.max(x[:, t : t + 128].reshape(32, 8, 128), axis=0)
                        top = y if top is None else jnp.maximum(top, y)
                top_ref[h] = top
    spot = lax.broadcasted_iota(jnp.int32, (1, 128), 1)
    out = jnp.zeros((1, 128), jnp.float32)
    for h in range(heads):
        best = jnp.max(jnp.max(top_ref[h], axis=0, keepdims=True), axis=1, keepdims=True)
        out = jnp.where(spot == h, best, out)
    out = out * (1.0 / wire_scale) * HEAD ** (-0.5)
    o_ref[...] = jnp.broadcast_to(out[:, :heads].reshape(1, 1, heads), o_ref.shape)


def local_maxima(a, w, kv, kw, seg, copies):
    cosine, sine = rope_tables()
    heads = kw.shape[1] // NOPE
    vmem = pl.BlockSpec(memory_space=pltpu.VMEM)
    return pl.pallas_call(
        maxima_kernel,
        out_shape=jax.ShapeDtypeStruct((copies, 1, heads), jnp.float32),
        in_specs=[vmem] * 7,
        out_specs=vmem,
        scratch_shapes=[
            pltpu.VMEM((SEQ, 4 * HEAD), jnp.float32),
            pltpu.VMEM((heads, 256, SEQ), jnp.bfloat16),
            pltpu.VMEM((SEQ, SEQ), jnp.float32),
            pltpu.VMEM((heads, 8, 128), jnp.float32),
        ],
        compiler_params=pltpu.CompilerParams(vmem_limit_bytes=32 << 20),
    )(a, w, kv, kw, seg, jnp.asarray(cosine), jnp.asarray(sine))


def finish_kernel(section_ref, all_ref, wq_ref, wk_ref, ratio_ref, sq_ref, sk_ref):
    layers, heads = ratio_ref.shape
    own = jnp.zeros((1, heads), jnp.float32)
    for s in range(layers):
        best = all_ref[s]
        for d in range(1, all_ref.shape[0] // layers):
            best = jnp.maximum(best, all_ref[d * layers + s])
        ratio_ref[s : s + 1, :] = best / clip_threshold
        own = jnp.where(section_ref[0] == s, best, own)
    factor = clip_threshold / jnp.maximum(own, clip_threshold)
    root = jnp.sqrt(factor)
    column = lax.broadcasted_iota(jnp.int32, (1, wq_ref.shape[1]), 1)
    scale = jnp.zeros((1, wq_ref.shape[1]), jnp.float32)
    for h in range(heads):
        scale = jnp.where(column >= h * HEAD, root[:, h : h + 1], scale)
        scale = jnp.where(column >= h * HEAD + NOPE, factor[:, h : h + 1], scale)
    sq_ref[...] = (wq_ref[...].astype(jnp.float32) * scale).astype(jnp.bfloat16)
    for h in range(heads):
        here = slice(h * NOPE, (h + 1) * NOPE)
        sk_ref[:, here] = (wk_ref[:, here].astype(jnp.float32) * root[:, h : h + 1]).astype(jnp.bfloat16)


def finish(section, everything, wq, wk, layers):
    vmem = pl.BlockSpec(memory_space=pltpu.VMEM)
    return pl.pallas_call(
        finish_kernel,
        out_shape=(
            jax.ShapeDtypeStruct((layers, everything.shape[2]), jnp.float32),
            jax.ShapeDtypeStruct(wq.shape, jnp.bfloat16),
            jax.ShapeDtypeStruct(wk.shape, jnp.bfloat16),
        ),
        in_specs=[pl.BlockSpec(memory_space=pltpu.SMEM), vmem, vmem, vmem],
        out_specs=(vmem, vmem, vmem),
    )(section, everything, wq, wk)


def per_device(q_latent, kv_latent, segment_ids, q_weight, k_weight):
    layers = lax.axis_size("section")
    copies = lax.axis_size("dp") * layers
    sent = (q_weight[0].astype(jnp.float32) * wire_scale).astype(jnp.float16)
    gathered = lax.all_gather(sent, "dp", axis=0, tiled=True).astype(jnp.bfloat16)
    kv = jnp.swapaxes(kv_latent[0], 0, 1)
    own = local_maxima(q_latent[0], gathered, kv, k_weight[0], segment_ids.reshape(1, -1), copies)
    everything = lax.all_to_all(own, ("dp", "section"), 0, 0, tiled=True)
    section = lax.axis_index("section").astype(jnp.int32).reshape(1)
    ratio, scaled_q, scaled_k = finish(section, everything, q_weight[0], k_weight[0], layers)
    return ratio, scaled_q[None], scaled_k[None]


def solution(mesh):
    return jax.shard_map(
        per_device,
        mesh=mesh,
        in_specs=(
            P("section", "dp", None),
            P("section", "dp", None),
            P("dp"),
            P("section", "dp", "head"),
            P("section", None, "head"),
        ),
        out_specs=(P(None, "head"), P("section", "dp", "head"), P("section", None, "head")),
        check_vma=False,
    )
```

time: 129 us -> 81 us (0.63)
  waiting for transfers between devices: 71.4 us -> 12.1 us
  blocking collectives: 15.3 us -> 48.9 us
  between operations: 14.1 us -> 0.68 us
  local copies, waits for them, and re-layouts: 10.8 us -> 1.72 us
  matrix products: 8.69 us -> 0 us
  Pallas kernels: 0 us -> 8.36 us
  starting transfers between devices: 4 us -> 7.13 us
  other arithmetic: 3.26 us -> 1.84 us
    all_gather x1 -> x0, waiting for transfers between devices: 68.6 us -> none  [per_device(): lax.all_gather(q_weight[0], 'dp', axis=0, tiled=True)]
    all_gather x0 -> x1, blocking collectives: none -> 48.9 us  [per_device(): lax.all_gather(sent, 'dp', axis=0, tiled=True).astype(jnp.bfloat16)]
    all_to_all x1 -> x0, blocking collectives: 15.3 us -> none  [copy_for_each(): lax.all_to_all(jnp.broadcast_to(value[None], (count, *value.shape)), axis...]
    all_to_all x1, waiting for transfers between devices: 2.13 us -> 12.1 us  [per_device(): everything = lax.all_to_all(own, ('dp', 'section'), 0, 0, tiled=True)]
    dot_general x3 -> x0, matrix products: 8.69 us -> none  [the longest x1 4.52 us: per_device(): jnp.dot(latent_q, lax.all_gather(q_weight[0], 'dp', axis=0, tiled=True),...]
    pallas_call x0 -> x2, Pallas kernels: none -> 8.36 us  [the longest x1 5.43 us: local_maxima(): pl.pallas_call(maxima_kernel, out_shape=jax.ShapeDtypeStruct((copies, 1,...]
    dot_general x1 -> x0, local copies, waits for them, and re-layouts: 6.7 us -> none  [per_device(): jnp.dot(latent_q, lax.all_gather(q_weight[0], 'dp', axis=0, tiled=True),...]
    all_to_all x1, starting transfers between devices: 3.97 us -> 7.13 us  [per_device(): everything = lax.all_to_all(own, ('dp', 'section'), 0, 0, tiled=True)]
  transfers between devices with their start and end apart: 2 -> 1, of which waited for: 2 -> 1; matrix products, arithmetic and copies ran while one was open for 5% -> 0% of each run, Pallas kernels for 0% -> 0%
where the time goes in v1:
time: 81 us; the launch traced here: 80.7 us
  blocking collectives  48.9 us (60%)
  waiting for transfers between devices  12.1 us (15%)
  Pallas kernels  8.36 us (10%)
  starting transfers between devices  7.13 us (9%)
  other arithmetic  1.84 us (2%)
  local copies, waits for them, and re-layouts  1.72 us (2%)
    all_gather x1, blocking collectives, per_device(): lax.all_gather(sent, 'dp', axis=0, tiled=True).astype(jnp.bfloat16)  48.9 us
    all_to_all x1, waiting for transfers between devices, per_device(): everything = lax.all_to_all(own, ('dp', 'section'), 0, 0, tiled=True)  12.1 us
    all_to_all x1, starting transfers between devices, per_device(): everything = lax.all_to_all(own, ('dp', 'section'), 0, 0, tiled=True)  7.13 us
    pallas_call x1, Pallas kernels, local_maxima(): pl.pallas_call(maxima_kernel, out_shape=jax.ShapeDtypeStruct((copies, 1,...  5.43 us
    pallas_call x1, Pallas kernels, finish(): pl.pallas_call(finish_kernel, out_shape=(jax.ShapeDtypeStruct((layers, ev...  2.93 us
    unnamed x14, local copies, waits for them, and re-layouts  1.72 us
  transfers between devices with their start and end apart: 1, of which 1 were waited for; matrix products, arithmetic and copies ran while one was open for 0% of the time, Pallas kernels for 0%

profile of v1, /device:TPU:1, one launch (start us, length us, event | category | flops | bytes accessed | tf_op | source)
XLA Modules:
  0.0 80.7 jit_solution(3360570768395722635)
XLA Ops:
  0.6 1.0 %multiply_convert_fusion = f16[64,1536]{1,0:T(8,128)(2,1)S(1)} fusion(bf16[1,64,1536]{2,1,0:T(8,128)(2,1)} %param.10), kind=kLoop, calls=%fused_computation | loop fusion | flops 294912 | bytes 393216 | tf_op jit(solution)/shard_map/convert_element_type | solution.py:143
  1.6 48.9 %all-gather.1 = f16[1536,1536]{1,0:T(8,128)(2,1)S(1)} all-gather(f16[64,1536]{1,0:T(8,128)(2,1)S(1)} %multiply_convert_fusion), channel_id=1, replica_groups=mesh['dp'=24,'section'=4,'head'=8] {'dp'}, dimensions={0}, use_global_device_ids=true | all-gather | bytes 4915200 | tf_op jit(solution)/shard_map/all_gather | solution.py:144
  50.5 0.0 copy-start
  50.5 0.0 copy-start.1
  50.5 0.0 copy-start.2
  50.5 0.0 copy-start.3
  50.5 0.0 copy-start.4
  50.5 0.0 copy-start.5
  50.6 0.9 %convert_element_type.11.w_ref = bf16[1536,1536]{1,0:T(8,128)(2,1)S(1)} convert(f16[1536,1536]{1,0:T(8,128)(2,1)S(1)} %all-gather.1) | non-fusion elementwise | flops 2359296 | bytes 9437184 | tf_op jit(solution)/shard_map/convert_element_type | solution.py:144
  51.4 0.3 copy-done
  51.7 0.5 copy-done.1
  52.3 0.1 copy-done.2
  52.4 0.1 copy-done.3
  52.4 0.1 copy-done.4
  52.5 0.0 copy-done.5
  52.5 5.4 %shard_map.94 = f32[96,1,8]{2,1,0:T(1,128)} custom-call(bf16[512,1536]{1,0:T(8,128)(2,1)S(1)} %bitcast.13, bf16[1536,1536]{1,0:T(8,128)(2,1)S(1)} %convert_element_type.11.w_ref, bf16[576,512]{1,0:T(8,128)(2,1)S(1)} %bitcast.14, bf16[512,1024]{1,0:T(8,128)(2,1)S(1)} %bitcast.12, s32[1,512]{1,0:T(1,128)S(1)} %bitcast.15, f32[512,128]{1,0:T(8,128)S(1)} %copy-done.3, ...), custom_call_target="tpu_custom_call" | custom-call | tf_op jit(solution)/shard_map/pallas_call | solution.py:89
  58.0 7.1 %all-to-all-start = ((f32[96,1,8]{2,1,0:T(1,128)}), f32[96,1,8]{2,1,0:T(1,128)S(1)}, u32[]{:S(2)}, u32[]{:S(2)}) async-start(f32[96,1,8]{2,1,0:T(1,128)} %shard_map.94), calls=%async_computation | async-start | bytes 98304 | tf_op jit(solution)/shard_map/all_to_all | solution.py:147
  65.1 12.1 %all-to-all-done.all_ref = f32[96,1,8]{2,1,0:T(1,128)S(1)} async-done(((f32[96,1,8]{2,1,0:T(1,128)}), f32[96,1,8]{2,1,0:T(1,128)S(1)}, u32[]{:S(2)}, u32[]{:S(2)}) %all-to-all-start) | async-done | bytes 3104 | tf_op jit(solution)/shard_map/all_to_all | solution.py:147
  77.2 0.0 copy-start.6
  77.2 0.6 copy-done.6
  77.8 2.9 %shard_map.95 = (f32[4,8]{1,0:T(4,128)}, bf16[64,1536]{1,0:T(8,128)(2,1)}, bf16[512,1024]{1,0:T(8,128)(2,1)}) custom-call(s32[1]{0:T(128)} %bitcast.section_ref, f32[96,1,8]{2,1,0:T(1,128)} %copy-done.6, bf16[64,1536]{1,0:T(8,128)(2,1)} %bitcast.16, bf16[512,1024]{1,0:T(8,128)(2,1)} %bitcast.11), custom_call_target="tpu_custom_call" | custom-call | tf_op jit(solution)/shard_map/pallas_call | solution.py:128
Async XLA Ops:
  50.5 1.2 %copy-start = (bf16[1,512,1024]{2,1,0:T(8,128)(2,1)S(1)}, bf16[1,512,1024]{2,1,0:T(8,128)(2,1)}, u32[]{:S(2)}) copy-start(bf16[1,512,1024]{2,1,0:T(8,128)(2,1)} %param.11) | copy-start | bytes 3145732
  50.5 1.7 %copy-start.1 = (bf16[1,512,1536]{2,1,0:T(8,128)(2,1)S(1)}, bf16[1,512,1536]{2,1,0:T(8,128)(2,1)}, u32[]{:S(2)}) copy-start(bf16[1,512,1536]{2,1,0:T(8,128)(2,1)} %param.7) | copy-start | bytes 4718596
  50.5 1.8 %copy-start.2 = (bf16[1,512,576]{1,2,0:T(8,128)(2,1)S(1)}, bf16[1,512,576]{1,2,0:T(8,128)(2,1)}, u32[]{:S(2)}) copy-start(bf16[1,512,576]{1,2,0:T(8,128)(2,1)} %param.8) | copy-start | bytes 1769476
  50.5 1.9 %copy-start.3 = (f32[512,128]{1,0:T(8,128)S(1)}, f32[512,128]{1,0:T(8,128)}, u32[]{:S(2)}) copy-start(f32[512,128]{1,0:T(8,128)} %constant.11.clone.cos_ref) | copy-start | bytes 786436
  50.5 2.0 %copy-start.4 = (f32[512,128]{1,0:T(8,128)S(1)}, f32[512,128]{1,0:T(8,128)}, u32[]{:S(2)}) copy-start(f32[512,128]{1,0:T(8,128)} %constant.12.clone.sin_ref) | copy-start | bytes 786436
  50.5 2.0 %copy-start.5 = (s32[512]{0:T(512)S(1)}, s32[512]{0:T(512)}, u32[]{:S(2)}) copy-start(s32[512]{0:T(512)} %param.9) | copy-start | bytes 6148
  58.0 19.2 %all-to-all-start = ((f32[96,1,8]{2,1,0:T(1,128)}), f32[96,1,8]{2,1,0:T(1,128)S(1)}, u32[]{:S(2)}, u32[]{:S(2)}) async-start(f32[96,1,8]{2,1,0:T(1,128)} %shard_map.94), calls=%async_computation | async-start | bytes 98304 | tf_op jit(solution)/shard_map/all_to_all | solution.py:147
  77.2 0.6 copy-start.6

commit v2 on v1

--- a/solution.py
+++ b/solution.py
@@ -134,6 +134,7 @@
         ),
         in_specs=[pl.BlockSpec(memory_space=pltpu.SMEM), vmem, vmem, vmem],
         out_specs=(vmem, vmem, vmem),
+        compiler_params=pltpu.CompilerParams(vmem_limit_bytes=8 << 20),
     )(section, everything, wq, wk)
 
 
@@ -141,11 +142,12 @@
     layers = lax.axis_size("section")
     copies = lax.axis_size("dp") * layers
     sent = (q_weight[0].astype(jnp.float32) * wire_scale).astype(jnp.float16)
+    section = lax.axis_index("section").astype(jnp.int32).reshape(1)
+    section, sent = lax.optimization_barrier((section, sent))
     gathered = lax.all_gather(sent, "dp", axis=0, tiled=True).astype(jnp.bfloat16)
     kv = jnp.swapaxes(kv_latent[0], 0, 1)
     own = local_maxima(q_latent[0], gathered, kv, k_weight[0], segment_ids.reshape(1, -1), copies)
     everything = lax.all_to_all(own, ("dp", "section"), 0, 0, tiled=True)
-    section = lax.axis_index("section").astype(jnp.int32).reshape(1)
     ratio, scaled_q, scaled_k = finish(section, everything, q_weight[0], k_weight[0], layers)
     return ratio, scaled_q[None], scaled_k[None]
 

time: 81 us -> 78.2 us (0.965)
  blocking collectives: 48.9 us -> 68 us
  waiting for transfers between devices: 12.1 us -> 0 us
  starting transfers between devices: 7.13 us -> 0 us
  Pallas kernels: 8.36 us -> 6.38 us
    all_to_all x0 -> x1, blocking collectives: none -> 19.1 us  [per_device(): everything = lax.all_to_all(own, ('dp', 'section'), 0, 0, tiled=True)]
    all_to_all x1 -> x0, waiting for transfers between devices: 12.1 us -> none  [per_device(): everything = lax.all_to_all(own, ('dp', 'section'), 0, 0, tiled=True)]
    all_to_all x1 -> x0, starting transfers between devices: 7.13 us -> none  [per_device(): everything = lax.all_to_all(own, ('dp', 'section'), 0, 0, tiled=True)]
    pallas_call x1, Pallas kernels: 2.93 us -> 1.58 us  [finish(): pl.pallas_call(finish_kernel, out_shape=(jax.ShapeDtypeStruct((layers, ev...]
  transfers between devices with their start and end apart: 1 -> 0, of which waited for: 1 -> 0; matrix products, arithmetic and copies ran while one was open for 0% -> 0% of each run, Pallas kernels for 0% -> 0%
where the time goes in v2:
time: 78.2 us; the launch traced here: 78 us
  blocking collectives  68 us (87%)
  Pallas kernels  6.38 us (8%)
  other arithmetic  1.84 us (2%)
  local copies, waits for them, and re-layouts  1.1 us (1%)
    all_gather x1, blocking collectives, per_device(): lax.all_gather(sent, 'dp', axis=0, tiled=True).astype(jnp.bfloat16)  48.9 us
    all_to_all x1, blocking collectives, per_device(): everything = lax.all_to_all(own, ('dp', 'section'), 0, 0, tiled=True)  19.1 us
    pallas_call x1, Pallas kernels, local_maxima(): pl.pallas_call(maxima_kernel, out_shape=jax.ShapeDtypeStruct((copies, 1,...  4.8 us
    pallas_call x1, Pallas kernels, finish(): pl.pallas_call(finish_kernel, out_shape=(jax.ShapeDtypeStruct((layers, ev...  1.58 us

profile of v2, /device:TPU:1, one launch (start us, length us, event | category | flops | bytes accessed | tf_op | source)
XLA Modules:
  0.0 78.0 jit_solution(9530506521714817697)
XLA Ops:
  0.6 1.0 %multiply_convert_fusion = f16[64,1536]{1,0:T(8,128)(2,1)S(1)} fusion(bf16[1,64,1536]{2,1,0:T(8,128)(2,1)} %param.10), kind=kLoop, calls=%fused_computation | loop fusion | flops 294912 | bytes 393216 | tf_op jit(solution)/shard_map/convert_element_type | solution.py:144
  1.6 48.9 %all-gather.1 = f16[1536,1536]{1,0:T(8,128)(2,1)S(1)} all-gather(f16[64,1536]{1,0:T(8,128)(2,1)S(1)} %multiply_convert_fusion), channel_id=1, replica_groups=mesh['dp'=24,'section'=4,'head'=8] {'dp'}, dimensions={0}, use_global_device_ids=true | all-gather | bytes 4915200 | tf_op jit(solution)/shard_map/all_gather | solution.py:147
  50.5 0.0 copy-start
  50.5 0.0 copy-start.1
  50.5 0.0 copy-start.3
  50.5 0.0 copy-start.4
  50.5 0.0 copy-start.5
  50.5 0.0 copy-start.6
  50.6 0.9 %convert_element_type.11.w_ref = bf16[1536,1536]{1,0:T(8,128)(2,1)S(1)} convert(f16[1536,1536]{1,0:T(8,128)(2,1)S(1)} %all-gather.1) | non-fusion elementwise | flops 2359296 | bytes 9437184 | tf_op jit(solution)/shard_map/convert_element_type | solution.py:147
  51.4 0.0 copy-start.2
  51.4 0.3 copy-done
  51.8 0.5 copy-done.1
  52.3 0.1 copy-done.3
  52.4 0.1 copy-done.4
  52.4 0.1 copy-done.5
  52.5 0.0 copy-done.6
  52.5 4.8 %shard_map.94 = f32[96,1,8]{2,1,0:T(1,128)S(1)} custom-call(bf16[512,1536]{1,0:T(8,128)(2,1)S(1)} %bitcast.13, bf16[1536,1536]{1,0:T(8,128)(2,1)S(1)} %convert_element_type.11.w_ref, bf16[576,512]{1,0:T(8,128)(2,1)S(1)} %bitcast.15, bf16[512,1024]{1,0:T(8,128)(2,1)S(1)} %bitcast.11, s32[1,512]{1,0:T(1,128)S(1)} %bitcast.16, f32[512,128]{1,0:T(8,128)S(1)} %copy-done.5, ...), custom_call_target="tpu_custom_call" | custom-call | tf_op jit(solution)/shard_map/pallas_call | solution.py:89
  57.3 19.1 %all_to_all.5.all_ref = f32[96,1,8]{2,1,0:T(1,128)S(1)} all-to-all(f32[96,1,8]{2,1,0:T(1,128)S(1)} %shard_map.94), channel_id=1, replica_groups=mesh['dp'=24,'section'=4,'head'=8] {'dp','section'}, dimensions={0} | all-to-all | bytes 6144 | tf_op jit(solution)/shard_map/all_to_all | solution.py:150
  76.4 0.0 copy-done.2
  76.4 1.6 %shard_map.95 = (f32[4,8]{1,0:T(4,128)}, bf16[64,1536]{1,0:T(8,128)(2,1)}, bf16[512,1024]{1,0:T(8,128)(2,1)}) custom-call(s32[1]{0:T(128)} %bitcast.section_ref, f32[96,1,8]{2,1,0:T(1,128)S(1)} %all_to_all.5.all_ref, bf16[64,1536]{1,0:T(8,128)(2,1)S(1)} %bitcast.14, bf16[512,1024]{1,0:T(8,128)(2,1)S(1)} %bitcast.12), custom_call_target="tpu_custom_call" | custom-call | tf_op jit(solution)/shard_map/pallas_call | solution.py:128
Async XLA Ops:
  50.5 1.2 %copy-start = (bf16[1,512,1024]{2,1,0:T(8,128)(2,1)S(1)}, bf16[1,512,1024]{2,1,0:T(8,128)(2,1)}, u32[]{:S(2)}) copy-start(bf16[1,512,1024]{2,1,0:T(8,128)(2,1)} %param.11) | copy-start | bytes 3145732
  50.5 1.7 %copy-start.1 = (bf16[1,512,1536]{2,1,0:T(8,128)(2,1)S(1)}, bf16[1,512,1536]{2,1,0:T(8,128)(2,1)}, u32[]{:S(2)}) copy-start(bf16[1,512,1536]{2,1,0:T(8,128)(2,1)} %param.7) | copy-start | bytes 4718596
  50.5 1.8 %copy-start.3 = (bf16[1,512,576]{1,2,0:T(8,128)(2,1)S(1)}, bf16[1,512,576]{1,2,0:T(8,128)(2,1)}, u32[]{:S(2)}) copy-start(bf16[1,512,576]{1,2,0:T(8,128)(2,1)} %param.8) | copy-start | bytes 1769476
  50.5 1.9 %copy-start.4 = (f32[512,128]{1,0:T(8,128)S(1)}, f32[512,128]{1,0:T(8,128)}, u32[]{:S(2)}) copy-start(f32[512,128]{1,0:T(8,128)} %constant.12.clone.sin_ref) | copy-start | bytes 786436
  50.5 2.0 %copy-start.5 = (f32[512,128]{1,0:T(8,128)S(1)}, f32[512,128]{1,0:T(8,128)}, u32[]{:S(2)}) copy-start(f32[512,128]{1,0:T(8,128)} %constant.11.clone.cos_ref) | copy-start | bytes 786436
  50.5 2.0 %copy-start.6 = (s32[512]{0:T(512)S(1)}, s32[512]{0:T(512)}, u32[]{:S(2)}) copy-start(s32[512]{0:T(512)} %param.9) | copy-start | bytes 6148
  51.4 25.0 %copy-start.2 = (bf16[1,64,1536]{2,1,0:T(8,128)(2,1)S(1)}, bf16[1,64,1536]{2,1,0:T(8,128)(2,1)}, u32[]{:S(2)}) copy-start(bf16[1,64,1536]{2,1,0:T(8,128)(2,1)} %param.10) | copy-start | bytes 589828

commit v3 on v2

--- a/solution.py
+++ b/solution.py
@@ -28,7 +28,7 @@
     return np.tile(cosine, (1, 4)), np.concatenate([-sine, sine, -sine, sine], 1)
 
 
-def maxima_kernel(a_ref, w_ref, kv_ref, kw_ref, seg_ref, cos_ref, sin_ref, o_ref, q_ref, kc_ref, bias_ref, top_ref):
+def maxima_kernel(q_ref, kv_ref, kw_ref, seg_ref, cos_ref, sin_ref, o_ref, kc_ref, bias_ref, top_ref):
     heads = kw_ref.shape[1] // NOPE
     lane = lax.broadcasted_iota(jnp.int32, (SEQ, 128), 1)
     low = lane < 64
@@ -51,10 +51,8 @@
         here = slice(j * 128, (j + 1) * 128)
         same = column == jnp.broadcast_to(row[:, here], (SEQ, 128))
         bias_ref[:, here] = jnp.where(same & (lane + j * 128 <= position), 0.0, masked)
-    width = 4 * HEAD
     for g in range(heads // 4):
-        q_ref[...] = jnp.dot(a_ref[...], w_ref[:, g * width : (g + 1) * width], preferred_element_type=jnp.float32)
-        for p in range(2):
+        for p in range(2 * g, 2 * g + 2):
             first = q_ref[:, p * 384 : p * 384 + 128]
             second = q_ref[:, p * 384 + 128 : p * 384 + 256]
             third = q_ref[:, p * 384 + 256 : p * 384 + 384]
@@ -63,7 +61,7 @@
             turned = (turn * cos_ref[...] + partner * sin_ref[...]).astype(jnp.bfloat16)
             swapped = jnp.where(low, third, second)
             for i, part in enumerate((first, swapped)):
-                h = 4 * g + 2 * p + i
+                h = 2 * p + i
                 query = jnp.concatenate([part.astype(jnp.bfloat16), turned], 1)
                 top = None
                 for s0, s1, t1 in ((0, 256, 256), (256, 512, 512)):
@@ -82,23 +80,22 @@
     o_ref[...] = jnp.broadcast_to(out[:, :heads].reshape(1, 1, heads), o_ref.shape)
 
 
-def local_maxima(a, w, kv, kw, seg, copies):
+def local_maxima(q, kv, kw, seg, copies):
     cosine, sine = rope_tables()
     heads = kw.shape[1] // NOPE
     vmem = pl.BlockSpec(memory_space=pltpu.VMEM)
     return pl.pallas_call(
         maxima_kernel,
         out_shape=jax.ShapeDtypeStruct((copies, 1, heads), jnp.float32),
-        in_specs=[vmem] * 7,
+        in_specs=[vmem] * 6,
         out_specs=vmem,
         scratch_shapes=[
-            pltpu.VMEM((SEQ, 4 * HEAD), jnp.float32),
             pltpu.VMEM((heads, 256, SEQ), jnp.bfloat16),
             pltpu.VMEM((SEQ, SEQ), jnp.float32),
             pltpu.VMEM((heads, 8, 128), jnp.float32),
         ],
-        compiler_params=pltpu.CompilerParams(vmem_limit_bytes=32 << 20),
-    )(a, w, kv, kw, seg, jnp.asarray(cosine), jnp.asarray(sine))
+        compiler_params=pltpu.CompilerParams(vmem_limit_bytes=16 << 20),
+    )(q, kv, kw, seg, jnp.asarray(cosine), jnp.asarray(sine))
 
 
 def finish_kernel(section_ref, all_ref, wq_ref, wk_ref, ratio_ref, sq_ref, sk_ref):
@@ -146,7 +143,8 @@
     section, sent = lax.optimization_barrier((section, sent))
     gathered = lax.all_gather(sent, "dp", axis=0, tiled=True).astype(jnp.bfloat16)
     kv = jnp.swapaxes(kv_latent[0], 0, 1)
-    own = local_maxima(q_latent[0], gathered, kv, k_weight[0], segment_ids.reshape(1, -1), copies)
+    q = jnp.dot(q_latent[0], gathered, preferred_element_type=jnp.float32)
+    own = local_maxima(q, kv, k_weight[0], segment_ids.reshape(1, -1), copies)
     everything = lax.all_to_all(own, ("dp", "section"), 0, 0, tiled=True)
     ratio, scaled_q, scaled_k = finish(section, everything, q_weight[0], k_weight[0], layers)
     return ratio, scaled_q[None], scaled_k[None]

time: 78.2 us -> 76.3 us (0.976)
  Pallas kernels: 6.38 us -> 3.68 us
  matrix products: 0 us -> 2.6 us
  local copies, waits for them, and re-layouts: 1.1 us -> 0.04 us
    pallas_call x1, Pallas kernels: 4.8 us -> 2.09 us  [local_maxima(): pl.pallas_call(maxima_kernel, out_shape=jax.ShapeDtypeStruct((copies, 1,...]
    dot_general x0 -> x1, matrix products: none -> 2.6 us  [per_device(): q = jnp.dot(q_latent[0], gathered, preferred_element_type=jnp.float32)]
    unnamed x14, local copies, waits for them, and re-layouts: 1.1 us -> 0.04 us
    convert_element_type x1 -> x0, other arithmetic: 0.87 us -> none  [per_device(): lax.all_gather(sent, 'dp', axis=0, tiled=True).astype(jnp.bfloat16)]
where the time goes in v3:
time: 76.3 us; the launch traced here: 76.2 us
  blocking collectives  68 us (89%)
  Pallas kernels  3.68 us (5%)
  matrix products  2.6 us (3%)
  other arithmetic  1.09 us (1%)
    all_gather x1, blocking collectives, per_device(): lax.all_gather(sent, 'dp', axis=0, tiled=True).astype(jnp.bfloat16)  48.9 us
    all_to_all x1, blocking collectives, per_device(): everything = lax.all_to_all(own, ('dp', 'section'), 0, 0, tiled=True)  19.1 us
    dot_general x1, matrix products, per_device(): q = jnp.dot(q_latent[0], gathered, preferred_element_type=jnp.float32)  2.6 us
    pallas_call x1, Pallas kernels, local_maxima(): pl.pallas_call(maxima_kernel, out_shape=jax.ShapeDtypeStruct((copies, 1,...  2.09 us
    pallas_call x1, Pallas kernels, finish(): pl.pallas_call(finish_kernel, out_shape=(jax.ShapeDtypeStruct((layers, ev...  1.59 us

profile of v3, /device:TPU:1, one launch (start us, length us, event | category | flops | bytes accessed | tf_op | source)
XLA Modules:
  0.0 76.2 jit_solution(10357717049968036820)
XLA Ops:
  0.6 0.0 copy-start
  0.6 1.1 %multiply_convert_fusion = f16[64,1536]{1,0:T(8,128)(2,1)S(1)} fusion(bf16[1,64,1536]{2,1,0:T(8,128)(2,1)} %param.10), kind=kLoop, calls=%fused_computation.4 | loop fusion | flops 294912 | bytes 393216 | tf_op jit(solution)/shard_map/convert_element_type | solution.py:141
  1.7 48.9 %all-gather.1 = f16[1536,1536]{1,0:T(8,128)(2,1)S(1)} all-gather(f16[64,1536]{1,0:T(8,128)(2,1)S(1)} %multiply_convert_fusion), channel_id=1, replica_groups=mesh['dp'=24,'section'=4,'head'=8] {'dp'}, dimensions={0}, use_global_device_ids=true | all-gather | bytes 4915200 | tf_op jit(solution)/shard_map/all_gather | solution.py:144
  50.7 0.0 copy-done
  50.7 0.0 copy-start.1
  50.7 0.0 copy-start.3
  50.7 0.0 copy-start.4
  50.7 0.0 copy-start.5
  50.7 0.0 copy-start.6
  50.7 2.6 %fusion.2.q_ref = f32[512,1536]{1,0:T(8,128)S(1)} fusion(f16[1536,1536]{1,0:T(8,128)(2,1)S(1)} %all-gather.1, bf16[1,512,1536]{2,1,0:T(8,128)(2,1)S(1)} %copy-done), kind=kOutput, calls=%fused_computation.2 | convolution fusion | flops 2418278400 | bytes 9437184 | tf_op jit(solution)/shard_map/dot_general | solution.py:146
  53.3 0.0 copy-start.2
  53.3 0.0 copy-done.1
  53.3 0.0 copy-done.3
  53.3 0.0 copy-done.4
  53.3 0.0 copy-done.5
  53.4 0.0 copy-done.6
  53.4 2.1 %shard_map.94 = f32[96,1,8]{2,1,0:T(1,128)S(1)} custom-call(f32[512,1536]{1,0:T(8,128)S(1)} %fusion.2.q_ref, bf16[576,512]{1,0:T(8,128)(2,1)S(1)} %bitcast.18, bf16[512,1024]{1,0:T(8,128)(2,1)S(1)} %bitcast.15, s32[1,512]{1,0:T(1,128)S(1)} %bitcast.19, f32[512,128]{1,0:T(8,128)S(1)} %copy-done.5, f32[512,128]{1,0:T(8,128)S(1)} %copy-done.4), custom_call_target="tpu_custom_call" | custom-call | tf_op jit(solution)/shard_map/pallas_call | solution.py:87
  55.5 19.1 %all_to_all.5.all_ref = f32[96,1,8]{2,1,0:T(1,128)S(1)} all-to-all(f32[96,1,8]{2,1,0:T(1,128)S(1)} %shard_map.94), channel_id=1, replica_groups=mesh['dp'=24,'section'=4,'head'=8] {'dp','section'}, dimensions={0} | all-to-all | bytes 6144 | tf_op jit(solution)/shard_map/all_to_all | solution.py:148
  74.6 0.0 copy-done.2
  74.6 1.6 %shard_map.95 = (f32[4,8]{1,0:T(4,128)}, bf16[64,1536]{1,0:T(8,128)(2,1)}, bf16[512,1024]{1,0:T(8,128)(2,1)}) custom-call(s32[1]{0:T(128)} %bitcast.section_ref, f32[96,1,8]{2,1,0:T(1,128)S(1)} %all_to_all.5.all_ref, bf16[64,1536]{1,0:T(8,128)(2,1)S(1)} %bitcast.17, bf16[512,1024]{1,0:T(8,128)(2,1)S(1)} %bitcast.16), custom_call_target="tpu_custom_call" | custom-call | tf_op jit(solution)/shard_map/pallas_call | solution.py:125
Async XLA Ops:
  0.6 50.0 %copy-start = (bf16[1,512,1536]{2,1,0:T(8,128)(2,1)S(1)}, bf16[1,512,1536]{2,1,0:T(8,128)(2,1)}, u32[]{:S(2)}) copy-start(bf16[1,512,1536]{2,1,0:T(8,128)(2,1)} %param.7) | copy-start | bytes 4718596
  50.7 2.7 %copy-start.1 = (bf16[1,512,1024]{2,1,0:T(8,128)(2,1)S(1)}, bf16[1,512,1024]{2,1,0:T(8,128)(2,1)}, u32[]{:S(2)}) copy-start(bf16[1,512,1024]{2,1,0:T(8,128)(2,1)} %param.11) | copy-start | bytes 3145732
  50.7 2.7 %copy-start.3 = (bf16[1,512,576]{1,2,0:T(8,128)(2,1)S(1)}, bf16[1,512,576]{1,2,0:T(8,128)(2,1)}, u32[]{:S(2)}) copy-start(bf16[1,512,576]{1,2,0:T(8,128)(2,1)} %param.8) | copy-start | bytes 1769476
  50.7 2.7 %copy-start.4 = (f32[512,128]{1,0:T(8,128)S(1)}, f32[512,128]{1,0:T(8,128)}, u32[]{:S(2)}) copy-start(f32[512,128]{1,0:T(8,128)} %constant.12.clone.sin_ref) | copy-start | bytes 786436
  50.7 2.7 %copy-start.5 = (f32[512,128]{1,0:T(8,128)S(1)}, f32[512,128]{1,0:T(8,128)}, u32[]{:S(2)}) copy-start(f32[512,128]{1,0:T(8,128)} %constant.11.clone.cos_ref) | copy-start | bytes 786436
  50.7 2.7 %copy-start.6 = (s32[512]{0:T(512)S(1)}, s32[512]{0:T(512)}, u32[]{:S(2)}) copy-start(s32[512]{0:T(512)} %param.9) | copy-start | bytes 6148
  53.3 21.3 %copy-start.2 = (bf16[1,64,1536]{2,1,0:T(8,128)(2,1)S(1)}, bf16[1,64,1536]{2,1,0:T(8,128)(2,1)}, u32[]{:S(2)}) copy-start(bf16[1,64,1536]{2,1,0:T(8,128)(2,1)} %param.10) | copy-start | bytes 589828

commit v4 on v3

--- a/solution.py
+++ b/solution.py
@@ -98,15 +98,16 @@
     )(q, kv, kw, seg, jnp.asarray(cosine), jnp.asarray(sine))
 
 
-def finish_kernel(section_ref, all_ref, wq_ref, wk_ref, ratio_ref, sq_ref, sk_ref):
+def finish_kernel(all_ref, wq_ref, wk_ref, ratio_ref, sq_ref, sk_ref):
     layers, heads = ratio_ref.shape
+    section = lax.axis_index("section")
     own = jnp.zeros((1, heads), jnp.float32)
     for s in range(layers):
         best = all_ref[s]
         for d in range(1, all_ref.shape[0] // layers):
             best = jnp.maximum(best, all_ref[d * layers + s])
         ratio_ref[s : s + 1, :] = best / clip_threshold
-        own = jnp.where(section_ref[0] == s, best, own)
+        own = jnp.where(section == s, best, own)
     factor = clip_threshold / jnp.maximum(own, clip_threshold)
     root = jnp.sqrt(factor)
     column = lax.broadcasted_iota(jnp.int32, (1, wq_ref.shape[1]), 1)
@@ -120,7 +121,7 @@
         sk_ref[:, here] = (wk_ref[:, here].astype(jnp.float32) * root[:, h : h + 1]).astype(jnp.bfloat16)
 
 
-def finish(section, everything, wq, wk, layers):
+def finish(everything, wq, wk, layers):
     vmem = pl.BlockSpec(memory_space=pltpu.VMEM)
     return pl.pallas_call(
         finish_kernel,
@@ -129,24 +130,22 @@
             jax.ShapeDtypeStruct(wq.shape, jnp.bfloat16),
             jax.ShapeDtypeStruct(wk.shape, jnp.bfloat16),
         ),
-        in_specs=[pl.BlockSpec(memory_space=pltpu.SMEM), vmem, vmem, vmem],
+        in_specs=[vmem, vmem, vmem],
         out_specs=(vmem, vmem, vmem),
         compiler_params=pltpu.CompilerParams(vmem_limit_bytes=8 << 20),
-    )(section, everything, wq, wk)
+    )(everything, wq, wk)
 
 
 def per_device(q_latent, kv_latent, segment_ids, q_weight, k_weight):
     layers = lax.axis_size("section")
     copies = lax.axis_size("dp") * layers
     sent = (q_weight[0].astype(jnp.float32) * wire_scale).astype(jnp.float16)
-    section = lax.axis_index("section").astype(jnp.int32).reshape(1)
-    section, sent = lax.optimization_barrier((section, sent))
     gathered = lax.all_gather(sent, "dp", axis=0, tiled=True).astype(jnp.bfloat16)
     kv = jnp.swapaxes(kv_latent[0], 0, 1)
     q = jnp.dot(q_latent[0], gathered, preferred_element_type=jnp.float32)
     own = local_maxima(q, kv, k_weight[0], segment_ids.reshape(1, -1), copies)
     everything = lax.all_to_all(own, ("dp", "section"), 0, 0, tiled=True)
-    ratio, scaled_q, scaled_k = finish(section, everything, q_weight[0], k_weight[0], layers)
+    ratio, scaled_q, scaled_k = finish(everything, q_weight[0], k_weight[0], layers)
     return ratio, scaled_q[None], scaled_k[None]
 
 

time: 76.3 us -> 76.3 us (level)
  no operation moved by 1% of the time
where the time goes in v4:
time: 76.3 us; the launch traced here: 76.2 us
  blocking collectives  68 us (89%)
  Pallas kernels  3.68 us (5%)
  matrix products  2.6 us (3%)
  other arithmetic  1.09 us (1%)
    all_gather x1, blocking collectives, per_device(): lax.all_gather(sent, 'dp', axis=0, tiled=True).astype(jnp.bfloat16)  48.9 us
    all_to_all x1, blocking collectives, per_device(): everything = lax.all_to_all(own, ('dp', 'section'), 0, 0, tiled=True)  19.1 us
    dot_general x1, matrix products, per_device(): q = jnp.dot(q_latent[0], gathered, preferred_element_type=jnp.float32)  2.6 us
    pallas_call x1, Pallas kernels, local_maxima(): pl.pallas_call(maxima_kernel, out_shape=jax.ShapeDtypeStruct((copies, 1,...  2.09 us
    pallas_call x1, Pallas kernels, finish(): pl.pallas_call(finish_kernel, out_shape=(jax.ShapeDtypeStruct((layers, ev...  1.59 us

profile of v4, /device:TPU:1, one launch (start us, length us, event | category | flops | bytes accessed | tf_op | source)
XLA Modules:
  0.0 76.2 jit_solution(9946127975160111509)
XLA Ops:
  0.6 0.0 copy-start
  0.6 1.1 %multiply_convert_fusion = f16[64,1536]{1,0:T(8,128)(2,1)S(1)} fusion(bf16[1,64,1536]{2,1,0:T(8,128)(2,1)} %param.10), kind=kLoop, calls=%fused_computation.4 | loop fusion | flops 294912 | bytes 393216 | tf_op jit(solution)/shard_map/convert_element_type | solution.py:142
  1.7 48.9 %all-gather.1 = f16[1536,1536]{1,0:T(8,128)(2,1)S(1)} all-gather(f16[64,1536]{1,0:T(8,128)(2,1)S(1)} %multiply_convert_fusion), channel_id=1, replica_groups=mesh['dp'=24,'section'=4,'head'=8] {'dp'}, dimensions={0}, use_global_device_ids=true | all-gather | bytes 4915200 | tf_op jit(solution)/shard_map/all_gather | solution.py:143
  50.7 0.0 copy-done
  50.7 0.0 copy-start.1
  50.7 0.0 copy-start.3
  50.7 0.0 copy-start.4
  50.7 0.0 copy-start.5
  50.7 0.0 copy-start.6
  50.7 2.6 %fusion.2.q_ref = f32[512,1536]{1,0:T(8,128)S(1)} fusion(f16[1536,1536]{1,0:T(8,128)(2,1)S(1)} %all-gather.1, bf16[1,512,1536]{2,1,0:T(8,128)(2,1)S(1)} %copy-done), kind=kOutput, calls=%fused_computation.2 | convolution fusion | flops 2418278400 | bytes 9437184 | tf_op jit(solution)/shard_map/dot_general | solution.py:145
  53.3 0.0 copy-start.2
  53.3 0.0 copy-done.1
  53.3 0.0 copy-done.3
  53.3 0.0 copy-done.4
  53.3 0.0 copy-done.5
  53.4 0.0 copy-done.6
  53.4 2.1 %shard_map.94 = f32[96,1,8]{2,1,0:T(1,128)S(1)} custom-call(f32[512,1536]{1,0:T(8,128)S(1)} %fusion.2.q_ref, bf16[576,512]{1,0:T(8,128)(2,1)S(1)} %bitcast.17, bf16[512,1024]{1,0:T(8,128)(2,1)S(1)} %bitcast.14, s32[1,512]{1,0:T(1,128)S(1)} %bitcast.18, f32[512,128]{1,0:T(8,128)S(1)} %copy-done.5, f32[512,128]{1,0:T(8,128)S(1)} %copy-done.4), custom_call_target="tpu_custom_call" | custom-call | tf_op jit(solution)/shard_map/pallas_call | solution.py:87
  55.5 19.1 %all_to_all.5.all_ref = f32[96,1,8]{2,1,0:T(1,128)S(1)} all-to-all(f32[96,1,8]{2,1,0:T(1,128)S(1)} %shard_map.94), channel_id=1, replica_groups=mesh['dp'=24,'section'=4,'head'=8] {'dp','section'}, dimensions={0} | all-to-all | bytes 6144 | tf_op jit(solution)/shard_map/all_to_all | solution.py:147
  74.6 0.0 copy-done.2
  74.6 1.6 %shard_map.95 = (f32[4,8]{1,0:T(4,128)}, bf16[64,1536]{1,0:T(8,128)(2,1)}, bf16[512,1024]{1,0:T(8,128)(2,1)}) custom-call(f32[96,1,8]{2,1,0:T(1,128)S(1)} %all_to_all.5.all_ref, bf16[64,1536]{1,0:T(8,128)(2,1)S(1)} %bitcast.16, bf16[512,1024]{1,0:T(8,128)(2,1)S(1)} %bitcast.15), custom_call_target="tpu_custom_call" | custom-call | tf_op jit(solution)/shard_map/pallas_call | solution.py:126
Async XLA Ops:
  0.6 50.0 %copy-start = (bf16[1,512,1536]{2,1,0:T(8,128)(2,1)S(1)}, bf16[1,512,1536]{2,1,0:T(8,128)(2,1)}, u32[]{:S(2)}) copy-start(bf16[1,512,1536]{2,1,0:T(8,128)(2,1)} %param.7) | copy-start | bytes 4718596
  50.7 2.7 %copy-start.1 = (bf16[1,512,1024]{2,1,0:T(8,128)(2,1)S(1)}, bf16[1,512,1024]{2,1,0:T(8,128)(2,1)}, u32[]{:S(2)}) copy-start(bf16[1,512,1024]{2,1,0:T(8,128)(2,1)} %param.11) | copy-start | bytes 3145732
  50.7 2.7 %copy-start.3 = (bf16[1,512,576]{1,2,0:T(8,128)(2,1)S(1)}, bf16[1,512,576]{1,2,0:T(8,128)(2,1)}, u32[]{:S(2)}) copy-start(bf16[1,512,576]{1,2,0:T(8,128)(2,1)} %param.8) | copy-start | bytes 1769476
  50.7 2.7 %copy-start.4 = (f32[512,128]{1,0:T(8,128)S(1)}, f32[512,128]{1,0:T(8,128)}, u32[]{:S(2)}) copy-start(f32[512,128]{1,0:T(8,128)} %constant.7.clone.sin_ref) | copy-start | bytes 786436
  50.7 2.7 %copy-start.5 = (f32[512,128]{1,0:T(8,128)S(1)}, f32[512,128]{1,0:T(8,128)}, u32[]{:S(2)}) copy-start(f32[512,128]{1,0:T(8,128)} %constant.6.clone.cos_ref) | copy-start | bytes 786436
  50.7 2.7 %copy-start.6 = (s32[512]{0:T(512)S(1)}, s32[512]{0:T(512)}, u32[]{:S(2)}) copy-start(s32[512]{0:T(512)} %param.9) | copy-start | bytes 6148
  53.3 21.3 %copy-start.2 = (bf16[1,64,1536]{2,1,0:T(8,128)(2,1)S(1)}, bf16[1,64,1536]{2,1,0:T(8,128)(2,1)}, u32[]{:S(2)}) copy-start(bf16[1,64,1536]{2,1,0:T(8,128)(2,1)} %param.10) | copy-start | bytes 589828
